TPU v7x, 32 devices: a whole 2x2x4 slice. The times are simulated.
32 devices in a mesh: branch: 4 (over z), row: 4 (over y, core), col: 2 (over x).
Axes of the slice: x: 2, y: 2, z: 4, core: 2. Of those that a mesh axis runs over, the one named last changes fastest.
Arguments:
- homolog_tensor: bfloat16 [64, 128, 256], P('col', 'row'), may hold values from -6 to 6
- couple_tensor: bfloat16 [128, 128, 128], P('row', 'col'), may hold values from -6 to 6
- probe_matrix: bfloat16 [256, 256], P(None, 'branch'), may hold values from -0.375 to 0.375
- lookup_matrix: bfloat16 [256, 256], P(None, 'branch'), may hold values from -0.375 to 0.375
- content_matrix: bfloat16 [256, 256], P(None, 'branch'), may hold values from -0.375 to 0.375
- scoring_sigmoid_matrix: bfloat16 [256, 256], P(None, 'branch'), may hold values from -0.375 to 0.375
- scoring_final_matrix: bfloat16 [256, 256], P('branch'), may hold values from -0.375 to 0.375
- couple_offset_matrix: bfloat16 [128, 8], P(None, 'branch'), may hold values from -43 to 43
- product_first_matrix: bfloat16 [256, 32], replicated, may hold values from -0.375 to 0.375
- product_second_matrix: bfloat16 [256, 32], replicated, may hold values from -0.375 to 0.375
- product_final_matrix: bfloat16 [1024, 128], replicated, may hold values from -1 to 1
- trio_first_matrix: bfloat16 [2, 128, 128], P(None, None, 'branch'), may hold values from -0.5 to 0.5
- trio_second_matrix: bfloat16 [2, 128, 128], P(None, None, 'branch'), may hold values from -0.5 to 0.5
- trio_sigmoid_matrix: bfloat16 [128, 128], replicated, may hold values from -0.5 to 0.5
- trio_final_matrix: bfloat16 [128, 128], replicated, may hold values from -0.5 to 0.5
Outputs:
- revised_homolog_matrix: bfloat16 [64, 128, 256], P('col', 'row', 'branch')
- pairwise_output: bfloat16 [128, 128, 128], P('row', 'col')
All inputs are finite; a program needn't handle non-finite values.
Results may differ from a plain program's by a relative error of at most 0.014.
Values may be sent and summed in bfloat16 or wider, within the bound.
No kernel may reach another device: no remote copies, remote signals or barrier semaphores. Data moves between devices by JAX's collectives and lax.ppermute only.
A program may use at most 64 MiB of HBM per device.

v0:
```python
import jax
import jax.numpy as jnp
from jax import lax
from jax.sharding import PartitionSpec as P

EPS = 1e-05


def spread_2(block, axis, owner):
    block = jnp.where(lax.axis_index(axis) == owner, block, jnp.zeros_like(block))
    return lax.psum(block, axis)


def standardise_rows(values):
    values = values.astype(jnp.float32)
    centred = values - jnp.mean(values, axis=-1, keepdims=True)
    variance = jnp.mean(centred * centred, axis=-1, keepdims=True)
    return centred / jnp.sqrt(variance + EPS)


def apply_linear(source, weights):
    return jnp.dot(
        source.reshape(-1, weights.shape[0]), weights, preferred_element_type=jnp.float32
    )


def attend(query, key, value, bias):
    scale = float(query.shape[-1]) ** (-0.5)
    scores = jnp.einsum("sihd,sjhd->shij", query, key, preferred_element_type=jnp.float32) * scale
    scores = scores + jnp.transpose(bias, (2, 0, 1)).astype(jnp.float32)[None]
    top = jnp.max(scores, axis=-1, keepdims=True)
    expo = jnp.exp(scores - top)
    total = jnp.sum(expo, axis=-1)
    summed = jnp.einsum(
        "shij,sjhd->sihd", expo.astype(jnp.bfloat16), value, preferred_element_type=jnp.float32
    )
    return summed / jnp.transpose(total, (0, 2, 1))[..., None]


def per_device(
    homolog_tensor,
    couple_tensor,
    probe_matrix,
    lookup_matrix,
    content_matrix,
    scoring_sigmoid_matrix,
    scoring_final_matrix,
    couple_offset_matrix,
    product_first_matrix,
    product_second_matrix,
    product_final_matrix,
    trio_first_matrix,
    trio_second_matrix,
    trio_sigmoid_matrix,
    trio_final_matrix,
):
    branches = lax.axis_size("branch")
    rows_count = lax.axis_size("row")
    cols_count = lax.axis_size("col")
    quadrant_share = lax.axis_index("branch")
    col_index = lax.axis_index("col")
    homolog_share, position_tile, channel_extent = homolog_tensor.shape
    c_block = couple_tensor.shape[1]
    residues = position_tile * rows_count
    depth = probe_matrix.shape[1]
    local_heads = couple_offset_matrix.shape[1]
    head_size = depth // local_heads
    q_rows = position_tile // branches
    total_rows = homolog_share * cols_count
    outer_width = product_first_matrix.shape[1]
    standardised_tensor = standardise_rows(homolog_tensor).astype(jnp.bfloat16)
    pair_normed = standardise_rows(couple_tensor).astype(jnp.bfloat16)
    bias_tile = (
        apply_linear(pair_normed, couple_offset_matrix)
        .astype(jnp.bfloat16)
        .reshape(position_tile, c_block, local_heads)
    )
    bias_band = lax.all_gather(bias_tile, "col", axis=1, tiled=True)
    spread = lax.all_to_all(standardised_tensor, "row", split_axis=0, concat_axis=1, tiled=True)
    few = spread.shape[0]
    shaped = (few, residues, local_heads, head_size)
    query = apply_linear(spread, probe_matrix).astype(jnp.bfloat16).reshape(shaped)
    key = apply_linear(spread, lookup_matrix).astype(jnp.bfloat16).reshape(shaped)
    value = apply_linear(spread, content_matrix).astype(jnp.bfloat16).reshape(shaped)
    gate_pre = apply_linear(spread, scoring_sigmoid_matrix).reshape(shaped)
    bias_full = lax.all_gather(bias_band, "row", axis=0, tiled=True)
    attended_values = attend(query, key, value, bias_full) * jax.nn.sigmoid(gate_pre)
    attended_values = attended_values.astype(jnp.bfloat16).reshape(few, residues, depth)
    attended_values = lax.all_to_all(
        attended_values, "row", split_axis=1, concat_axis=0, tiled=True
    )
    joined_tensor = apply_linear(attended_values, scoring_final_matrix).reshape(
        homolog_share, position_tile, channel_extent
    )
    joined_tensor = lax.psum_scatter(
        joined_tensor.astype(jnp.bfloat16), "branch", scatter_dimension=2, tiled=True
    ).astype(jnp.float32)
    device_share = channel_extent // branches
    local_alignment = lax.dynamic_slice_in_dim(
        homolog_tensor, quadrant_share * device_share, device_share, 2
    )
    revised_homolog_matrix = (local_alignment.astype(jnp.float32) + joined_tensor).astype(
        jnp.bfloat16
    )
    left_rows = lax.dynamic_slice_in_dim(standardised_tensor, quadrant_share * q_rows, q_rows, 1)
    left_outer = (
        apply_linear(left_rows, product_first_matrix)
        .astype(jnp.bfloat16)
        .reshape(homolog_share, q_rows * outer_width)
    )
    right_local = (
        apply_linear(standardised_tensor, product_second_matrix)
        .astype(jnp.bfloat16)
        .reshape(homolog_share, position_tile, outer_width)
    )
    right_outer = lax.all_gather(right_local, "row", axis=1, tiled=True)
    wide_out = product_final_matrix.astype(jnp.float32)
    left_major = jnp.transpose(left_outer)
    count = lax.axis_size("col") * c_block
    piece = right_outer.reshape(homolog_share, count * outer_width)
    outer = jnp.dot(left_major, piece, preferred_element_type=jnp.float32)
    outer = outer.reshape(q_rows, outer_width, count, outer_width)
    outer = jnp.transpose(outer, (2, 0, 1, 3)).reshape(count * q_rows, outer_width * outer_width)
    term = jnp.dot(outer, wide_out, precision=lax.Precision.HIGHEST) / total_rows
    update = lax.psum_scatter(
        term.reshape(count, q_rows, wide_out.shape[1]).astype(jnp.bfloat16),
        "col",
        scatter_dimension=0,
        tiled=True,
    ).astype(jnp.float32)
    update = jnp.transpose(update, (1, 0, 2))
    pair_rows = lax.dynamic_slice_in_dim(couple_tensor, quadrant_share * q_rows, q_rows, 0)
    mid_rows = (pair_rows.astype(jnp.float32) + update).astype(jnp.bfloat16)
    pair_mid = lax.all_gather(mid_rows, "branch", axis=0, tiled=True)
    tri_normed = standardise_rows(pair_mid).astype(jnp.bfloat16)

    def gated(weights):
        linear = apply_linear(tri_normed, weights[0])
        opening = apply_linear(tri_normed, weights[1])
        return (
            (jax.nn.sigmoid(opening) * linear)
            .astype(jnp.bfloat16)
            .reshape(position_tile, c_block, weights.shape[2])
        )

    tri_left = gated(trio_first_matrix)
    tri_right = gated(trio_second_matrix)
    left_band, right_band = (
        lax.all_gather(tri_left, "col", axis=1, tiled=True),
        lax.all_gather(tri_right, "col", axis=1, tiled=True),
    )
    ratio = rows_count // cols_count

    def mirror(offset):
        return spread_2(right_band, "row", col_index * ratio + offset)

    right_cols = jnp.concatenate([mirror(offset) for offset in range(ratio)], axis=0)
    product = jnp.einsum("ikc,jkc->ijc", left_band, right_cols, preferred_element_type=jnp.float32)
    product = lax.all_to_all(product, "branch", split_axis=0, concat_axis=2, tiled=True)
    product_normed = standardise_rows(product).astype(jnp.bfloat16)
    own_normed = lax.dynamic_slice_in_dim(tri_normed, quadrant_share * q_rows, q_rows, 0)
    closing = jax.nn.sigmoid(apply_linear(own_normed, trio_sigmoid_matrix)).reshape(
        q_rows, c_block, -1
    )
    change = apply_linear(product_normed, trio_final_matrix).reshape(q_rows, c_block, -1)
    out_rows = (mid_rows.astype(jnp.float32) + closing * change).astype(jnp.bfloat16)
    pairwise_output = lax.all_gather(out_rows, "branch", axis=0, tiled=True)
    return (revised_homolog_matrix, pairwise_output)


def solution(mesh):
    return jax.shard_map(
        per_device,
        mesh=mesh,
        in_specs=(
            P("col", "row", None),
            P("row", "col", None),
            P(None, "branch"),
            P(None, "branch"),
            P(None, "branch"),
            P(None, "branch"),
            P("branch", None),
            P(None, "branch"),
            P(),
            P(),
            P(),
            P(None, None, "branch"),
            P(None, None, "branch"),
            P(),
            P(),
        ),
        out_specs=(P("col", "row", "branch"), P("row", "col", None)),
        check_vma=False,
    )
```

profile of v0, /device:TPU:0, one launch (start us, length us, event | category | flops | bytes accessed | tf_op | source)
XLA Modules:
  0.0 214.5 jit_solution(585322599231288311)
XLA Ops:
  8.0 1.3 convert_reduce_fusion.2
  9.3 1.4 fusion.35
  10.8 2.2 %fusion.36 = bf16[32,32,256]{2,1,0:T(8,128)(2,1)} fusion(bf16[32,32,256]{2,1,0:T(8,128)(2,1)} %param.15, f32[32,32]{1,0:T(8,128)S(1)} %add_sqrt_fusion.2, f32[32,32]{1,0:T(8,128)S(1)} %broadcast_multiply_fusion.2), kind=kLoop, calls=%fused_computation.61 | loop fusion | flops 1048576 | bytes 1056768 | tf_op jit(solution)/shard_map/convert_element_type | solution.py:71
  12.9 4.3 %all-to-all-start = ((bf16[32,32,256]{2,1,0:T(8,128)(2,1)}), bf16[32,32,256]{2,1,0:T(8,128)(2,1)S(1)}, u32[]{:S(2)}, u32[]{:S(2)}) async-start(bf16[32,32,256]{2,1,0:T(8,128)(2,1)} %fusion.36), calls=%async_computation | async-start | bytes 1048576 | tf_op jit(solution)/shard_map/all_to_all | solution.py:79
  17.2 1.1 convolution_convert_fusion.6
  18.7 1.3 convolution_convert_fusion.5
  20.2 12.4 %all_gather.23 = bf16[32,128,32]{2,1,0:T(8,128)(2,1)S(1)} all-gather(bf16[32,32,32]{2,1,0:T(8,128)(2,1)S(1)} %bitcast.167), channel_id=1, replica_groups=mesh['branch'=4,'row'=4,'col'=2] {'row'}, dimensions={1}, use_global_device_ids=true | all-gather | bytes 327680 | tf_op jit(solution)/shard_map/all_gather | solution.py:116
  32.5 1.1 reshape.160
  33.7 0.8 dot_general.90
  34.5 0.5 copy.80
  35.0 2.6 %convolution_bitcast_fusion = f32[128,8,32,32]{0,2,3,1:T(8,128)} fusion(bf16[8,32,32,1]{2,1,3,0:T(8,128)(2,1)S(1)} %bitcast.173, bf16[128,32,32]{0,2,1:T(8,128)(2,1)S(1)} %copy.80), kind=kOutput, calls=%fused_computation.13 | convolution fusion | flops 67108864 | bytes 4472832 | tf_op jit(solution)/shard_map/dot_general | solution.py:121
  37.6 14.4 %copy.81 = f32[128,8,32,32]{3,2,1,0:T(8,128)} copy(f32[128,8,32,32]{0,2,3,1:T(8,128)} %convolution_bitcast_fusion) | data formatting | bytes 8388608 | tf_op jit(solution)/shard_map/transpose | solution.py:123
  52.0 13.7 %reshape.161 = f32[1024,1024]{1,0:T(8,128)} reshape(f32[128,8,32,32]{3,2,1,0:T(8,128)} %copy.81) | data formatting | bytes 8388608 | tf_op jit(solution)/shard_map/reshape | solution.py:123
  65.8 4.2 %fusion.16 = bf16[128,8,128]{2,1,0:T(8,128)(2,1)S(1)} fusion(f32[1024,1024]{1,0:T(8,128)} %reshape.161, bf16[1024,128]{1,0:T(8,128)(2,1)S(1)} %copy-done), kind=kOutput, calls=%fused_computation.32 | convolution fusion | flops 1610874880 | bytes 4718592 | tf_op jit(solution)/shard_map/dot_general | solution.py:124
  70.0 0.7 copy.82
  70.7 0.3 convert_reduce_fusion.1
  71.1 0.6 fusion.33
  71.8 0.6 fusion.34
  72.9 4.7 %all_gather.21 = bf16[32,128,2]{0,2,1:T(2,128)(2,1)S(1)} all-gather(bf16[32,64,2]{0,2,1:T(2,128)(2,1)S(1)} %copy.69), channel_id=1, replica_groups=mesh['branch'=4,'row'=4,'col'=2] {'col'}, dimensions={1}, use_global_device_ids=true | all-gather | bytes 24576 | tf_op jit(solution)/shard_map/all_gather | solution.py:78
  77.7 5.4 %all_gather.22 = bf16[128,128,2]{1,2,0:T(2,128)(2,1)S(1)} all-gather(bf16[32,128,2]{1,2,0:T(2,128)(2,1)S(1)} %copy.70), channel_id=1, replica_groups=mesh['branch'=4,'row'=4,'col'=2] {'row'}, dimensions={0}, use_global_device_ids=true | all-gather | bytes 81920 | tf_op jit(solution)/shard_map/all_gather | solution.py:86
  83.3 0.3 fusion.30
  83.6 0.3 fusion.29
  83.9 0.3 fusion.28
  84.2 0.4 fusion.67
  84.8 0.3 fusion.22
  85.1 0.3 fusion.26
  85.6 0.9 reshape.175
  86.5 3.3 %all-to-all-start.1 = ((bf16[4,2,8192]{2,1,0:T(2,128)(2,1)}), bf16[4,2,8192]{2,1,0:T(2,128)(2,1)S(1)}, u32[]{:S(2)}, u32[]{:S(2)}) async-start(bf16[4,2,8192]{2,1,0:T(2,128)(2,1)} %reshape.175), calls=%async_computation.1 | async-start | bytes 262144 | tf_op jit(solution)/shard_map/all_to_all | solution.py:89
  89.9 4.5 %all-to-all-done.1 = bf16[4,2,8192]{2,1,0:T(2,128)(2,1)S(1)} async-done(((bf16[4,2,8192]{2,1,0:T(2,128)(2,1)}), bf16[4,2,8192]{2,1,0:T(2,128)(2,1)S(1)}, u32[]{:S(2)}, u32[]{:S(2)}) %all-to-all-start.1) | async-done | bytes 131104 | tf_op jit(solution)/shard_map/all_to_all | solution.py:89
  94.7 0.9 fusion.48
  95.6 16.2 %all_gather.24 = bf16[32,64,128]{2,1,0:T(8,128)(2,1)S(1)} all-gather(bf16[8,64,128]{2,1,0:T(8,128)(2,1)S(1)} %fusion.48), channel_id=1, replica_groups=mesh['branch'=4,'row'=4,'col'=2] {'branch'}, dimensions={0}, use_global_device_ids=true | all-gather | bytes 655360 | tf_op jit(solution)/shard_map/all_gather | solution.py:134
  111.8 0.3 convert_reduce_fusion
  112.2 0.6 fusion.31
  112.9 0.6 fusion.32
  113.5 0.3 fusion.2
  113.8 0.3 fusion.5
  114.1 0.3 fusion.6
  114.4 0.2 reshape.165
  114.6 0.9 copy.83
  115.5 12.4 %all_gather.25 = bf16[32,128,32]{2,0,1:T(8,128)(2,1)S(1)} all-gather(bf16[32,64,32]{2,0,1:T(8,128)(2,1)S(1)} %copy.83), channel_id=1, replica_groups=mesh['branch'=4,'row'=4,'col'=2] {'col'}, dimensions={1}, use_global_device_ids=true | all-gather | bytes 393216 | tf_op jit(solution)/shard_map/all_gather | solution.py:150
  127.9 1.3 copy.84
  129.3 0.8 broadcast_select_fusion.1
  130.1 0.3 fusion.7
  130.4 0.2 reshape.166
  130.6 0.9 copy.86
  131.5 11.6 %all_gather.26 = bf16[32,128,32]{2,0,1:T(8,128)(2,1)S(1)} all-gather(bf16[32,64,32]{2,0,1:T(8,128)(2,1)S(1)} %copy.86), channel_id=1, replica_groups=mesh['branch'=4,'row'=4,'col'=2] {'col'}, dimensions={1}, use_global_device_ids=true | all-gather | bytes 393216 | tf_op jit(solution)/shard_map/all_gather | solution.py:149
  143.1 1.3 copy.87
  144.4 18.6 %all-reduce.3.cloned.1.call-done = (bf16[32,128,32]{1,0,2:T(8,128)(2,1)}, bf16[32,128,32]{1,0,2:T(8,128)(2,1)}) async-done(((bf16[32,128,32]{1,0,2:T(8,128)(2,1)}, bf16[32,128,32]{1,0,2:T(8,128)(2,1)}), (bf16[32,128,32]{1,0,2:T(8,128)(2,1)}, bf16[32,128,32]{1,0,2:T(8,128)(2,1)})) %all-reduce.3.cloned.1.call-update) | async-done | bytes 524304 | tf_op jit(solution)/shard_map/psum | solution.py:11
  163.0 1.4 convolution_bitcast_fusion.1
  164.4 0.3 copy.116
  164.8 1.0 reshape.177
  165.8 4.6 %all-to-all-start.2 = ((f32[4,1,16384]{2,1,0:T(1,128)}), f32[4,1,16384]{2,1,0:T(1,128)}, u32[]{:S(2)}, u32[]{:S(2)}) async-start(f32[4,1,16384]{2,1,0:T(1,128)} %reshape.177), calls=%async_computation.3 | async-start | bytes 524288 | tf_op jit(solution)/shard_map/all_to_all | solution.py:159
  170.4 1.0 convolution_convert_fusion.1
  171.4 3.0 %copy.98 = bf16[32,32,256]{1,0,2:T(8,128)(2,1)S(1)} copy(bf16[32,32,256]{2,1,0:T(8,128)(2,1)S(1)} %convolution_convert_fusion.1) | data formatting | bytes 1048576
  174.4 2.9 %reshape.173 = bf16[256,1024]{1,0:T(8,128)(2,1)} reshape(bf16[256,32,32]{2,1,0:T(8,128)(2,1)S(1)} %bitcast.150) | data formatting | bytes 1048576
  177.4 1.0 fusion.25
  178.6 0.5 broadcast.127
  179.1 2.3 %reduce.2 = f32[4,16384]{1,0:T(4,128)S(1)} reduce(f32[4,1,16384]{2,1,0:T(1,128)} %all-to-all-done.2, f32[]{:T(128)} %broadcast.127), dimensions={1}, to_apply=%all_to_all.41.reduce_sub_computation | reduce | bytes 524292 | tf_op jit(solution)/shard_map/all_to_all | solution.py:159
  181.4 0.3 reshape.178
  182.3 21.3 %all_gather.27 = bf16[32,64,128]{2,1,0:T(8,128)(2,1)S(1)} all-gather(bf16[8,64,128]{2,1,0:T(8,128)(2,1)S(1)} %fusion.27), channel_id=1, replica_groups=mesh['branch'=4,'row'=4,'col'=2] {'branch'}, dimensions={0}, use_global_device_ids=true | all-gather | bytes 655360 | tf_op jit(solution)/shard_map/all_gather | solution.py:167
  203.5 1.3 reshape.174
  204.8 0.6 copy.99
  205.4 0.9 add_convert_fusion
  206.3 0.8 copy.120
  (64 shorter events, 2.8 us)
Async XLA Ops:
  8.0 57.7 %copy-start = (bf16[1024,128]{1,0:T(8,128)(2,1)S(1)}, bf16[1024,128]{1,0:T(8,128)(2,1)}, u32[]{:S(2)}) copy-start(bf16[1024,128]{1,0:T(8,128)(2,1)} %param.25) | copy-start | bytes 786436
  12.9 70.3 %all-to-all-start = ((bf16[32,32,256]{2,1,0:T(8,128)(2,1)}), bf16[32,32,256]{2,1,0:T(8,128)(2,1)S(1)}, u32[]{:S(2)}, u32[]{:S(2)}) async-start(bf16[32,32,256]{2,1,0:T(8,128)(2,1)} %fusion.36), calls=%async_computation | async-start | bytes 1048576 | tf_op jit(solution)/shard_map/all_to_all | solution.py:79
  17.2 77.5 %reduce-scatter.5.cloned.1.call-start = ((), (), s32[]{:S(2)}) async-start(), calls=%async_computation.5 | async-start | bytes 393216 | tf_op jit(solution)/shard_map/reduce_scatter | solution.py:125
  65.7 5.0 %copy-start.2 = (bf16[32,64,128]{2,1,0:T(8,128)(2,1)S(1)}, bf16[32,64,128]{2,1,0:T(8,128)(2,1)}, u32[]{:S(2)}) copy-start(bf16[32,64,128]{2,1,0:T(8,128)(2,1)} %param.16) | copy-start | bytes 1572868
  65.7 6.7 %copy-start.9 = (bf16[128,2]{0,1:T(2,128)(2,1)S(1)}, bf16[128,2]{0,1:T(2,128)(2,1)}, u32[]{:S(2)}) copy-start(bf16[128,2]{0,1:T(2,128)(2,1)} %param.22) | copy-start | bytes 1540
  65.7 17.5 %copy-start.4 = (bf16[256,64]{0,1:T(8,128)(2,1)S(1)}, bf16[256,64]{0,1:T(8,128)(2,1)}, u32[]{:S(2)}) copy-start(bf16[256,64]{0,1:T(8,128)(2,1)} %param.18) | copy-start | bytes 98308
  69.9 13.7 %copy-start.5 = (bf16[256,64]{0,1:T(8,128)(2,1)S(1)}, bf16[256,64]{0,1:T(8,128)(2,1)}, u32[]{:S(2)}) copy-start(bf16[256,64]{0,1:T(8,128)(2,1)} %param.17) | copy-start | bytes 98308
  70.0 14.0 %copy-start.6 = (bf16[256,64]{0,1:T(8,128)(2,1)S(1)}, bf16[256,64]{0,1:T(8,128)(2,1)}, u32[]{:S(2)}) copy-start(bf16[256,64]{0,1:T(8,128)(2,1)} %param.19) | copy-start | bytes 98308
  83.1 2.0 copy-start.10
  84.8 28.7 %copy-start.8 = (bf16[2,128,32]{1,2,0:T(8,128)(2,1)S(1)}, bf16[2,128,32]{1,2,0:T(8,128)(2,1)}, u32[]{:S(2)}) copy-start(bf16[2,128,32]{1,2,0:T(8,128)(2,1)} %param.26) | copy-start | bytes 49156
  85.1 28.7 %copy-start.7 = (bf16[2,128,32]{1,2,0:T(8,128)(2,1)S(1)}, bf16[2,128,32]{1,2,0:T(8,128)(2,1)}, u32[]{:S(2)}) copy-start(bf16[2,128,32]{1,2,0:T(8,128)(2,1)} %param.27) | copy-start | bytes 49156
  86.5 7.9 %all-to-all-start.1 = ((bf16[4,2,8192]{2,1,0:T(2,128)(2,1)}), bf16[4,2,8192]{2,1,0:T(2,128)(2,1)S(1)}, u32[]{:S(2)}, u32[]{:S(2)}) async-start(bf16[4,2,8192]{2,1,0:T(2,128)(2,1)} %reshape.175), calls=%async_computation.1 | async-start | bytes 262144 | tf_op jit(solution)/shard_map/all_to_all | solution.py:89
  89.8 73.2 %all-reduce.3.cloned.1.call-start = ((), (), s32[]{:S(2)}) async-start(), calls=%async_computation.7 | async-start | bytes 1048576 | tf_op jit(solution)/shard_map/psum | solution.py:11
  165.8 12.8 %all-to-all-start.2 = ((f32[4,1,16384]{2,1,0:T(1,128)}), f32[4,1,16384]{2,1,0:T(1,128)}, u32[]{:S(2)}, u32[]{:S(2)}) async-start(f32[4,1,16384]{2,1,0:T(1,128)} %reshape.177), calls=%async_computation.3 | async-start | bytes 524288 | tf_op jit(solution)/shard_map/all_to_all | solution.py:159
  170.4 33.1 %reduce-scatter.7.cloned.1.call-start = ((), (), s32[]{:S(2)}) async-start(), calls=%async_computation.6 | async-start | bytes 655360
  174.4 7.6 %copy-start.3 = (bf16[128,128]{1,0:T(8,128)(2,1)S(1)}, bf16[128,128]{1,0:T(8,128)(2,1)}, u32[]{:S(2)}) copy-start(bf16[128,128]{1,0:T(8,128)(2,1)} %param.29) | copy-start | bytes 98308
  177.4 28.0 %copy-start.1 = (bf16[32,32,256]{2,1,0:T(8,128)(2,1)S(1)}, bf16[32,32,256]{2,1,0:T(8,128)(2,1)}, u32[]{:S(2)}) copy-start(bf16[32,32,256]{2,1,0:T(8,128)(2,1)} %param.15) | copy-start | bytes 1572868
Sparse Core Ops, SparseCore 0:
  70.9 12.6 reduce-scatter.4
  130.2 32.7 all-reduce.2
Sparse Core Ops, SparseCore 1:
  177.5 25.9 reduce-scatter.6
where the time goes:
time: 215 us
  blocking collectives  83.9 us (39%)
  local copies, waits for them, and re-layouts  49.4 us (23%)
  waiting for transfers between devices  23.4 us (11%)
  between operations  16.1 us (7%)
  matrix products  16 us (7%)
  other arithmetic  13.5 us (6%)
  starting transfers between devices  12.2 us (6%)
    all_gather x1, blocking collectives, per_device(): pairwise_output = lax.all_gather(out_rows, 'branch', axis=0, tiled=True)  21.3 us
    psum x1, waiting for transfers between devices, spread_2(): return lax.psum(block, axis)  18.6 us
    all_gather x1, blocking collectives, per_device(): pair_mid = lax.all_gather(mid_rows, 'branch', axis=0, tiled=True)  16.2 us
    transpose x1, local copies, waits for them, and re-layouts, per_device(): jnp.transpose(outer, (2, 0, 1, 3))  14.4 us
    reshape x1, local copies, waits for them, and re-layouts, per_device(): jnp.transpose(outer, (2, 0, 1, 3))  13.7 us
    all_gather x1, blocking collectives, per_device(): lax.all_gather(tri_right, 'col', axis=1, tiled=True)  12.4 us
    all_gather x1, blocking collectives, per_device(): right_outer = lax.all_gather(right_local, 'row', axis=1, tiled=True)  12.4 us
    all_gather x1, blocking collectives, per_device(): lax.all_gather(tri_left, 'col', axis=1, tiled=True)  11.6 us
  transfers between devices with their start and end apart: 6, of which 3 were waited for; matrix products, arithmetic and copies ran while one was open for 28% of the time, Pallas kernels for 0%

commit v1 on v0

--- a/solution.py
+++ b/solution.py
@@ -1,6 +1,10 @@
+import functools
+
 import jax
 import jax.numpy as jnp
 from jax import lax
+from jax.experimental import pallas as pl
+from jax.experimental.pallas import tpu as pltpu
 from jax.sharding import PartitionSpec as P
 
 EPS = 1e-05
@@ -37,7 +41,7 @@
     return summed / jnp.transpose(total, (0, 2, 1))[..., None]
 
 
-def per_device(
+def plain_per_device(
     homolog_tensor,
     couple_tensor,
     probe_matrix,
@@ -168,9 +172,504 @@
     return (revised_homolog_matrix, pairwise_output)
 
 
+F32 = jnp.float32
+BF16 = jnp.bfloat16
+AXES = ("branch", "row", "col")
+LANES = 128
+HALF = LANES // 2
+QUART = LANES // 4
+
+
+def lane_of(shape):
+    return lax.broadcasted_iota(jnp.int32, shape, len(shape) - 1)
+
+
+def roll(x, shift):
+    shift %= x.shape[-1]
+    return pltpu.roll(x, shift, x.ndim - 1) if shift else x
+
+
+def dot_nn(a, b):
+    return jnp.dot(a, b, preferred_element_type=F32)
+
+
+def dot_nt(a, b):
+    return lax.dot_general(a, b, (((1,), (1,)), ((), ())), preferred_element_type=F32)
+
+
+def call(body, outs, scratch=(), flops=0, n_in=None, name=None):
+    return pl.pallas_call(
+        body,
+        out_shape=tuple(jax.ShapeDtypeStruct(s, d) for s, d in outs),
+        scratch_shapes=[pltpu.VMEM(s, d) for s, d in scratch],
+        compiler_params=pltpu.CompilerParams(vmem_limit_bytes=56 * 2**20),
+        cost_estimate=pl.CostEstimate(flops=flops, bytes_accessed=2**19, transcendentals=0),
+        name=name,
+    )
+
+
+def project_body(rows, hom, left_w, right_w, normed, left_t, right_t, scr):
+    n_rows, depth = hom.shape
+    share = n_rows // rows
+    width = left_w.shape[1]
+    step = 8
+    for first in range(0, share, step):
+        x = hom[first * rows : (first + step) * rows, :].astype(F32)
+        x = x - jnp.mean(x, axis=-1, keepdims=True)
+        x = x * lax.rsqrt(jnp.mean(x * x, axis=-1, keepdims=True) + EPS)
+        normed[first * rows : (first + step) * rows, :] = x.astype(BF16)
+        for s in range(step):
+            piece = x[s * rows : (s + 1) * rows, :]
+            for part in range(depth // LANES):
+                scr[part, pl.ds(first + s, rows, stride=share), :] = piece[
+                    :, part * LANES : (part + 1) * LANES
+                ]
+    w_l = jnp.transpose(left_w[...].astype(F32)).astype(BF16)
+    w_r = jnp.transpose(right_w[...].astype(F32)).astype(BF16)
+    weights = jnp.concatenate([w_l, w_r], axis=0)
+    acc = 0
+    for part in range(depth // LANES):
+        acc = acc + dot_nt(
+            weights[:, part * LANES : (part + 1) * LANES], scr[part].astype(BF16)
+        )
+    left_t[...] = acc[:width].astype(BF16)
+    right_t[...] = acc[width:].astype(BF16)
+
+
+def heads_body(normed, weights, kv, qg):
+    depth = weights.shape[1] // 2
+    full = dot_nn(normed[...], weights[...])
+    kv[...] = full[:, :depth].astype(BF16)
+    qg[...] = full[:, depth:]
+
+
+def pair_body(local_heads, width, couple, offset_t, outer_w, couple_t, bias, outer_wt, scr, wscr):
+    tiles = couple.shape[0] // LANES
+    for t in range(tiles):
+        x = jnp.transpose(couple[t * LANES : (t + 1) * LANES, :].astype(F32))
+        couple_t[t] = x.astype(BF16)
+        x = x - jnp.mean(x, axis=0, keepdims=True)
+        x = x * lax.rsqrt(jnp.mean(x * x, axis=0, keepdims=True) + EPS)
+        scr[pl.ds(t, offset_t.shape[0], stride=tiles), :] = dot_nn(offset_t[...], x.astype(BF16))
+    bias[...] = scr[: local_heads * tiles, :].astype(BF16)
+    wscr[...] = outer_w[...].astype(F32)
+    per = LANES // width
+    for g in range(width // per):
+        block = jnp.concatenate(
+            [wscr[pl.ds(g * per + q, width, stride=width), :] for q in range(per)], axis=0
+        )
+        outer_wt[:, g * LANES : (g + 1) * LANES] = jnp.transpose(block).astype(BF16)
+
+
+def gate_pair(x, w_lin, w_open):
+    return jax.nn.sigmoid(dot_nn(w_open, x)) * dot_nn(w_lin, x)
+
+
+def store_gated(scr, t, rows, gated):
+    chans = gated.shape[0] // 2
+    low = lane_of((chans, LANES)) < HALF
+    a, b = gated[:chans], gated[chans:]
+    scr[pl.ds(2 * t, chans, stride=rows), :] = jnp.where(low, a, roll(b, HALF))
+    scr[pl.ds(2 * t + 1, chans, stride=rows), :] = jnp.where(low, roll(a, HALF), b)
+
+
+def outer_body(
+    total_rows, couple_t, outer_wt, left_own, left_far, p_one, p_two, s_one, s_two, w_own, w_far,
+    mid_t, norm_t, right_pk, lhs, rscr, mscr, gscr,
+):
+    col = lax.axis_index("col")
+    row = lax.axis_index("row")
+    chip_y, core = row // 2, row % 2
+    width, span = left_own.shape
+    tiles = couple_t.shape[0]
+    rows = 2 * tiles
+    share = span // rows
+    block = rows * 2
+    group = lane_of((width, LANES)) // share
+    own_first = col == 0
+    for g in range(span // LANES):
+        cut = slice(g * LANES, (g + 1) * LANES)
+        own, far = left_own[:, cut].astype(F32), left_far[:, cut].astype(F32)
+        a, b = jnp.where(own_first, own, far), jnp.where(own_first, far, own)
+        even = jnp.where(
+            group == 0, a,
+            jnp.where(group == 1, roll(b, QUART), jnp.where(group == 2, roll(a, QUART), roll(b, HALF))),
+        )
+        odd = jnp.where(
+            group == 0, roll(a, HALF),
+            jnp.where(group == 1, roll(b, -QUART), jnp.where(group == 2, roll(a, -QUART), b)),
+        )
+        lhs[2 * g * width : (2 * g + 1) * width, :] = even.astype(BF16)
+        lhs[(2 * g + 1) * width : (2 * g + 2) * width, :] = odd.astype(BF16)
+    first_one = chip_y == 0
+    for a in range(2):
+        mine = core == a
+        for g in range(span // LANES):
+            cut = slice(g * LANES, (g + 1) * LANES)
+            one = jnp.where(mine, p_one[:, cut].astype(F32), s_one[:, cut].astype(F32))
+            two = jnp.where(mine, p_two[:, cut].astype(F32), s_two[:, cut].astype(F32))
+            t0, t1 = jnp.where(first_one, one, two), jnp.where(first_one, two, one)
+            for j4 in range(LANES // share):
+                j = a * rows + g * (LANES // share) + j4
+                tile = jnp.where(
+                    group == 0, roll(t0, -share * j4),
+                    jnp.where(group == 1, roll(t1, share - share * j4), 0.0),
+                )
+                rscr[pl.ds(j, width, stride=2 * block), :] = tile
+                rscr[pl.ds(block + j, width, stride=2 * block), :] = roll(tile, HALF)
+    left = lhs[...]
+    for q in range(0, width, 2):
+        rhs = rscr[q * LANES : (q + 2) * LANES, :].astype(BF16)
+        prod = dot_nt(left, rhs).astype(BF16)
+        for t in range(tiles):
+            for e in range(2):
+                mscr[t, (q + e) * width : (q + e + 1) * width, :] = prod[
+                    t * width : (t + 1) * width, e * LANES : (e + 1) * LANES
+                ]
+    w_lin = jnp.concatenate([w_own[2], w_far[2]], axis=0)
+    w_open = jnp.concatenate([w_own[3], w_far[3]], axis=0)
+    for t in range(0, tiles, 2):
+        both = dot_nn(outer_wt[...], jnp.concatenate([mscr[t], mscr[t + 1]], axis=1))
+        for e in range(2):
+            update = both[:, e * LANES : (e + 1) * LANES] * (1.0 / total_rows)
+            mid = (couple_t[t + e].astype(F32) + update).astype(BF16)
+            mid_t[t + e] = mid
+            x = mid.astype(F32)
+            x = x - jnp.mean(x, axis=0, keepdims=True)
+            x = x * lax.rsqrt(jnp.mean(x * x, axis=0, keepdims=True) + EPS)
+            x = x.astype(BF16)
+            norm_t[t + e] = x
+            store_gated(gscr, t + e, rows, gate_pair(x, w_lin, w_open))
+    right_pk[...] = gscr[...].astype(BF16)
+
+
+def left_body(norm_t, w_own, w_far, close_w, left_pk, close_t, gscr):
+    tiles = norm_t.shape[0]
+    w_lin = jnp.concatenate([w_own[0], w_far[0]], axis=0)
+    w_open = jnp.concatenate([w_own[1], w_far[1]], axis=0)
+    w_close = jnp.transpose(close_w[...].astype(F32)).astype(BF16)
+    for t in range(tiles):
+        x = norm_t[t]
+        store_gated(gscr, t, 2 * tiles, gate_pair(x, w_lin, w_open))
+        close_t[t] = jax.nn.sigmoid(dot_nn(w_close, x))
+    left_pk[...] = gscr[...].astype(BF16)
+
+
+def triangle_body(rows, left_pk, own, sib, across, across_sib, mine, other):
+    col = lax.axis_index("col")
+    row = lax.axis_index("row")
+    chip_y, core = row // 2, row % 2
+    is_low, here = core == 0, chip_y == col
+    low = lane_of((rows, LANES)) < HALF
+    for ch in range(left_pk.shape[0] // rows):
+        cut = slice(ch * rows, (ch + 1) * rows)
+        a = left_pk[cut, :]
+        zero = jnp.zeros_like(a)
+        lhs = jnp.concatenate([jnp.where(low, a, zero), jnp.where(low, zero, a)], axis=0)
+        o, s, x, xs = own[cut, :], sib[cut, :], across[cut, :], across_sib[cut, :]
+        n0, n1 = jnp.where(is_low, o, s), jnp.where(is_low, s, o)
+        f0, f1 = jnp.where(is_low, x, xs), jnp.where(is_low, xs, x)
+        rhs = jnp.concatenate(
+            [
+                jnp.where(here, n0, f0), jnp.where(here, n1, f1),
+                jnp.where(here, f0, n0), jnp.where(here, f1, n1),
+            ],
+            axis=0,
+        )
+        prod = dot_nt(lhs, rhs)
+        u, v = prod[:rows], prod[rows:]
+        mine[cut, :] = jnp.where(low, u, roll(v, HALF))
+        other[cut, :] = jnp.where(low, roll(u, HALF), v).astype(BF16)
+
+
+def final_body(rows, half_own, half_far, mid_t, close_t, final_w, out, scr, blocks):
+    branch = lax.axis_index("branch")
+    chans = half_own.shape[0] // rows
+    count = 4 * chans
+    low = lane_of((chans, LANES)) < HALF
+    parts = [half_own[...].astype(F32), half_far[...].astype(F32)]
+    parts = [p.reshape(chans, rows, LANES) for p in parts]
+    total = jnp.sum(parts[0], axis=0) + jnp.sum(parts[1], axis=0)
+    mean = (total + roll(total, HALF)) * (1.0 / count)
+    parts = [p - mean[None] for p in parts]
+    square = jnp.sum(parts[0] * parts[0], axis=0) + jnp.sum(parts[1] * parts[1], axis=0)
+    scale = lax.rsqrt((square + roll(square, HALF)) * (1.0 / count) + EPS)
+    for h in range(2):
+        scr[h] = (parts[h] * scale[None]).reshape(chans * rows, LANES)
+    w_t = jnp.transpose(final_w[...].astype(F32)).astype(BF16)
+    owners = [branch, branch ^ 2, branch ^ 1, branch ^ 3]
+    for t in range(rows // 2):
+        for h in range(2):
+            z0 = scr[h, pl.ds(2 * t, chans, stride=rows), :]
+            z1 = scr[h, pl.ds(2 * t + 1, chans, stride=rows), :]
+            first = jnp.where(low, z0, roll(z1, HALF))
+            second = jnp.where(low, roll(z0, HALF), z1)
+            for e, block in enumerate((first, second)):
+                at = pl.multiple_of(owners[2 * h + e] * chans, chans)
+                blocks[t % 2, pl.ds(at, chans), :] = block
+        change = dot_nn(w_t, blocks[t % 2].astype(BF16))
+        result = mid_t[t].astype(F32) + close_t[t] * change
+        out[t * LANES : (t + 1) * LANES, :] = jnp.transpose(result).astype(BF16)
+
+
+def attend_body(rows, head, qg, own, sib, across, across_sib, bias_own, bias_far, w_out, *rest):
+    outs, (bscr, cscr) = rest[:-2], rest[-2:]
+    col = lax.axis_index("col")
+    row = lax.axis_index("row")
+    branch = lax.axis_index("branch")
+    chip_y, core = row // 2, row % 2
+    is_low, top = core == 0, chip_y == 0
+    share = qg.shape[0] // rows
+    scale = float(head) ** (-0.5)
+    b_own, b_far = bias_own[...].astype(F32), bias_far[...].astype(F32)
+    b0, b1 = jnp.where(col == 0, b_own, b_far), jnp.where(col == 0, b_far, b_own)
+    n_bias = b0.shape[0]
+    low = lane_of((n_bias, LANES)) < HALF
+    bscr[pl.ds(0, n_bias, stride=2), :] = jnp.where(low, b0, roll(b1, HALF))
+    bscr[pl.ds(1, n_bias, stride=2), :] = jnp.where(low, roll(b0, HALF), b1)
+    bias = bscr[...]
+    lane = lane_of((rows, LANES))
+
+    def one(s):
+        cut = pl.ds(pl.multiple_of(s * rows, rows), rows)
+        o, b, x, xs = own[cut, :], sib[cut, :], across[cut, :], across_sib[cut, :]
+        n0, n1 = jnp.where(is_low, o, b), jnp.where(is_low, b, o)
+        f0, f1 = jnp.where(is_low, x, xs), jnp.where(is_low, xs, x)
+        kv = jnp.concatenate(
+            [
+                jnp.where(top, n0, f0), jnp.where(top, n1, f1),
+                jnp.where(top, f0, n0), jnp.where(top, f1, n1),
+            ],
+            axis=0,
+        )
+        both = qg[cut, :]
+        q = both.astype(BF16)
+        zero = jnp.zeros_like(q)
+        qm = jnp.concatenate(
+            [
+                jnp.where(lane < head, q, zero),
+                jnp.where((lane >= head) & (lane < 2 * head), q, zero),
+            ],
+            axis=0,
+        )
+        scores = dot_nt(qm, kv) * scale + bias
+        expo = jnp.exp(scores - jnp.max(scores, axis=-1, keepdims=True))
+        total = jnp.sum(expo, axis=-1, keepdims=True)
+        ctx = dot_nn(expo.astype(BF16), kv) / total
+        ctx = jnp.where(lane < 3 * head, ctx[:rows], ctx[rows:])
+        return ctx * jax.nn.sigmoid(both)
+
+    half = share // 2
+
+    def pair(s, carry):
+        first, second = one(s), one(s + half)
+        packed = jnp.where(lane < HALF, roll(first, HALF), second)
+        cscr[pl.ds(pl.multiple_of(s * rows, rows), rows), :] = packed.astype(BF16)
+        return carry
+
+    lax.fori_loop(0, half, pair, 0, unroll=2)
+    ctx = cscr[...]
+    for m in range(len(outs)):
+        outs[m][...] = dot_nn(ctx, w_out[branch ^ m]).astype(BF16)
+
+
+def revise_body(hom, p0, p1, p2, p3, out):
+    branch = lax.axis_index("branch")
+    acc = p0[...].astype(F32) + p1[...].astype(F32)
+    acc = acc + p2[...].astype(F32) + p3[...].astype(F32)
+    n = acc.shape[0]
+    at = pl.multiple_of((branch // 2) * LANES, LANES)
+    base = hom[:, pl.ds(at, LANES)].astype(F32)
+    base = jnp.where(branch % 2 == 0, base, roll(base, HALF))
+    out[:n, :] = (acc + base[:n])[:, :HALF].astype(BF16)
+    out[n:, :] = (roll(acc, HALF) + base[n:])[:, :HALF].astype(BF16)
+
+
+def fast_per_device(
+    mesh,
+    homolog_tensor,
+    couple_tensor,
+    probe_matrix,
+    lookup_matrix,
+    content_matrix,
+    scoring_sigmoid_matrix,
+    scoring_final_matrix,
+    couple_offset_matrix,
+    product_first_matrix,
+    product_second_matrix,
+    product_final_matrix,
+    trio_first_matrix,
+    trio_second_matrix,
+    trio_sigmoid_matrix,
+    trio_final_matrix,
+):
+    n_b, n_r, n_c = (mesh.shape[a] for a in AXES)
+
+    def send(x, source):
+        pairs = []
+        for b in range(n_b):
+            for r in range(n_r):
+                for c in range(n_c):
+                    sb, sr, sc = source(b, r, c)
+                    pairs.append(((sb * n_r + sr) * n_c + sc, (b * n_r + r) * n_c + c))
+        return lax.ppermute(x, AXES, pairs)
+
+    def other_col(b, r, c):
+        return b, r, c ^ 1
+
+    def other_core(b, r, c):
+        return b, r ^ 1, c
+
+    def other_chip(b, r, c):
+        return b, r ^ 2, c
+
+    def turned(b, r, c):
+        return b, 2 * c + r % 2, r // 2
+
+    def turned_far(b, r, c):
+        return b, 2 * c + r % 2, (r // 2) ^ 1
+
+    share, rows, depth = homolog_tensor.shape
+    block = couple_tensor.shape[1]
+    chans = couple_tensor.shape[2]
+    width = product_first_matrix.shape[1]
+    heads_w = probe_matrix.shape[1]
+    local_heads = couple_offset_matrix.shape[1]
+    head = heads_w // local_heads
+    quarter = trio_first_matrix.shape[2]
+    tiles = rows * block // LANES
+    n_rows = share * rows
+    hom = homolog_tensor.reshape(n_rows, depth)
+    couple = couple_tensor.reshape(rows * block, chans)
+
+    normed, left_t, right_t = call(
+        functools.partial(project_body, rows),
+        [((n_rows, depth), BF16), ((width, n_rows), BF16), ((width, n_rows), BF16)],
+        [((depth // LANES, n_rows, LANES), F32)],
+        name="project",
+    )(hom, product_first_matrix, product_second_matrix)
+    p_one = send(right_t, turned)
+    p_two = send(right_t, turned_far)
+    left_far = send(left_t, other_col)
+
+    offset_t = jnp.pad(couple_offset_matrix.T, ((0, 8 - local_heads), (0, 0)))
+    couple_t, bias, outer_wt = call(
+        functools.partial(pair_body, local_heads, width),
+        [
+            ((tiles, chans, LANES), BF16),
+            ((local_heads * tiles, LANES), BF16),
+            ((chans, width * width), BF16),
+        ],
+        [((8 * tiles, LANES), F32), ((width * width, chans), F32)],
+        name="pair",
+    )(couple, offset_t, product_final_matrix)
+    qkvg_w = jnp.concatenate(
+        [lookup_matrix, content_matrix, probe_matrix, scoring_sigmoid_matrix], axis=1
+    )
+    kv, qg = call(
+        heads_body, [((n_rows, 2 * heads_w), BF16), ((n_rows, 2 * heads_w), F32)], name="heads"
+    )(normed, qkvg_w)
+    w_own = jnp.transpose(
+        jnp.concatenate([trio_first_matrix, trio_second_matrix], axis=0), (0, 2, 1)
+    )
+    w_far = send(w_own, lambda b, r, c: (b ^ 2, r, c))
+    s_one, s_two = send(p_one, other_core), send(p_two, other_core)
+
+    mid_t, norm_t, right_pk = call(
+        functools.partial(outer_body, share * n_c),
+        [
+            ((tiles, chans, LANES), BF16),
+            ((tiles, chans, LANES), BF16),
+            ((quarter * rows, LANES), BF16),
+        ],
+        [
+            ((tiles * width, LANES), BF16),
+            ((width * LANES, LANES), F32),
+            ((tiles, width * width, LANES), BF16),
+            ((quarter * rows, LANES), F32),
+        ],
+        name="outer",
+    )(couple_t, outer_wt, left_t, left_far, p_one, p_two, s_one, s_two, w_own, w_far)
+    right_x = send(right_pk, other_chip)
+    right_s = send(right_pk, other_core)
+    left_pk, close_t = call(
+        left_body,
+        [((quarter * rows, LANES), BF16), ((tiles, chans, LANES), F32)],
+        [((quarter * rows, LANES), F32)],
+        name="left",
+    )(norm_t, w_own, w_far, trio_sigmoid_matrix)
+    right_xs = send(right_x, other_core)
+
+    kv_x = send(kv, other_chip)
+    bias_far = send(bias, other_col)
+    kv_s = send(kv, other_core)
+    kv_xs = send(kv_x, other_core)
+
+    mine, other = call(
+        functools.partial(triangle_body, rows),
+        [((quarter * rows, LANES), F32), ((quarter * rows, LANES), BF16)],
+        name="triangle",
+    )(left_pk, right_pk, right_s, right_x, right_xs)
+    far = send(other, other_col)
+    half_own = (mine + far.astype(F32)).astype(BF16)
+    half_far = send(half_own, lambda b, r, c: (b ^ 1, r, c))
+
+    w4 = jnp.transpose(scoring_final_matrix.reshape(heads_w, n_b, depth // n_b), (1, 0, 2))
+    zero = jnp.zeros_like(w4)
+    w_out = jnp.concatenate(
+        [jnp.concatenate([w4, zero], axis=2), jnp.concatenate([zero, w4], axis=2)], axis=1
+    )
+    parts = call(
+        functools.partial(attend_body, rows, head),
+        [((n_rows // 2, LANES), BF16)] * n_b,
+        [((local_heads * rows, LANES), F32), ((n_rows // 2, LANES), BF16)],
+        name="attend",
+    )(qg, kv, kv_s, kv_x, kv_xs, bias, bias_far, w_out)
+    parts = [parts[0]] + [
+        send(parts[m], lambda b, r, c, m=m: (b ^ m, r, c)) for m in range(1, n_b)
+    ]
+    (revised,) = call(revise_body, [((n_rows, depth // n_b), BF16)], name="revise")(hom, *parts)
+
+    (pair_out,) = call(
+        functools.partial(final_body, rows),
+        [((rows * block, chans), BF16)],
+        [((2, quarter * rows, LANES), F32), ((2, chans, LANES), F32)],
+        name="final",
+    )(half_own, half_far, mid_t, close_t, trio_final_matrix)
+    return (
+        revised.reshape(share, rows, depth // n_b),
+        pair_out.reshape(rows, block, chans),
+    )
+
+
+def fits(mesh, args):
+    hom, couple = args[0], args[1]
+    share, rows, depth = hom.shape
+    return (
+        mesh.shape["branch"] == 4
+        and mesh.shape["row"] == 4
+        and mesh.shape["col"] == 2
+        and couple.shape[0] == rows
+        and couple.shape[1] == 2 * rows == HALF
+        and couple.shape[2] == LANES
+        and share == QUART
+        and args[2].shape[1] == HALF
+        and depth == 4 * HALF
+        and args[8].shape[1] == QUART
+        and args[11].shape[2] == QUART
+        and args[7].shape[1] == 2
+    )
+
+
+def dispatch(mesh, *args):
+    if fits(mesh, args):
+        return fast_per_device(mesh, *args)
+    return plain_per_device(*args)
+
+
 def solution(mesh):
     return jax.shard_map(
-        per_device,
+        functools.partial(dispatch, mesh),
         mesh=mesh,
         in_specs=(
             P("col", "row", None),

time: 215 us -> 99.8 us (0.46)
  blocking collectives: 83.9 us -> 0 us
  local copies, waits for them, and re-layouts: 49.4 us -> 8.28 us
  Pallas kernels: 0 us -> 39.1 us
  matrix products: 16 us -> 0 us
  between operations: 16.1 us -> 0.89 us
  other arithmetic: 13.5 us -> 2.68 us
  starting transfers between devices: 12.2 us -> 23 us
    all_gather x7 -> x0, blocking collectives: 83.9 us -> none  [the longest x1 21.3 us: per_device(): pairwise_output = lax.all_gather(out_rows, 'branch', axis=0, tiled=True)]
    pallas_call x0 -> x9, Pallas kernels: none -> 39.1 us  [the longest x1 11.1 us: fast_per_device(): call(functools.partial(attend_body, rows, head), [((n_rows // 2, LANES),...]
    ppermute x0 -> x18, waiting for transfers between devices: none -> 25.2 us  [send(): return lax.ppermute(x, AXES, pairs)]
    ppermute x0 -> x18, starting transfers between devices: none -> 23 us  [send(): return lax.ppermute(x, AXES, pairs)]
    psum x1 -> x0, waiting for transfers between devices: 18.6 us -> none  [spread_2(): return lax.psum(block, axis)]
    reshape x11 -> x2, local copies, waits for them, and re-layouts: 17.7 us -> 0.11 us  [fast_per_device(): scoring_final_matrix.reshape(heads_w, n_b, depth // n_b)]
    dot_general x19 -> x0, matrix products: 16 us -> none  [the longest x14 7.2 us: apply_linear(): jnp.dot(source.reshape(-1, weights.shape[0]), weights, preferred_element_...]
    transpose x2 -> x0, local copies, waits for them, and re-layouts: 14.8 us -> none  [the longest x1 14.4 us: per_device(): jnp.transpose(outer, (2, 0, 1, 3))]
  transfers between devices with their start and end apart: 6 -> 18, of which waited for: 3 -> 5; matrix products, arithmetic and copies ran while one was open for 28% -> 4% of each run, Pallas kernels for 0% -> 24%
where the time goes in v1:
time: 99.8 us; the launch traced here: 99.2 us
  Pallas kernels  39.1 us (39%)
  waiting for transfers between devices  25.2 us (25%)
  starting transfers between devices  23 us (23%)
  local copies, waits for them, and re-layouts  8.28 us (8%)
  other arithmetic  2.68 us (3%)
    ppermute x18, waiting for transfers between devices, send(): return lax.ppermute(x, AXES, pairs)  25.2 us
    ppermute x18, starting transfers between devices, send(): return lax.ppermute(x, AXES, pairs)  23 us
    pallas_call x1, Pallas kernels, fast_per_device(): call(functools.partial(attend_body, rows, head), [((n_rows // 2, LANES),...  11.1 us
    pallas_call x1, Pallas kernels, fast_per_device(): call(functools.partial(outer_body, share * n_c), [((tiles, chans, LANES),...  7.78 us
    unnamed x66, local copies, waits for them, and re-layouts  7.61 us
    pallas_call x1, Pallas kernels, fast_per_device(): call(functools.partial(final_body, rows), [((rows * block, chans), BF16)]...  3.76 us
    pallas_call x1, Pallas kernels, fast_per_device(): call(functools.partial(project_body, rows), [((n_rows, depth), BF16), ((w...  3.31 us
    pallas_call x1, Pallas kernels, fast_per_device(): call(functools.partial(triangle_body, rows), [((quarter * rows, LANES), F...  3.09 us
  transfers between devices with their start and end apart: 18, of which 5 were waited for; matrix products, arithmetic and copies ran while one was open for 4% of the time, Pallas kernels for 24%

profile of v1, /device:TPU:0, one launch (start us, length us, event | category | flops | bytes accessed | tf_op | source)
XLA Modules:
  0.0 99.2 jit_solution(5031550331604903895)
XLA Ops:
  0.6 1.5 %copy.23.left_w = bf16[256,32]{1,0:T(8,128)(2,1)} copy(bf16[256,32]{0,1:T(8,128)(2,1)} %param.23) | data formatting | bytes 32768 | tf_op args[8]
  2.1 0.7 copy.24.right_w
  2.8 3.3 %project.1 = (bf16[1024,256]{1,0:T(8,128)(2,1)}, bf16[32,1024]{1,0:T(8,128)(2,1)}, bf16[32,1024]{1,0:T(8,128)(2,1)}) custom-call(bf16[1024,256]{1,0:T(8,128)(2,1)} %bitcast.10, bf16[256,32]{1,0:T(8,128)(2,1)} %copy.23.left_w, bf16[256,32]{1,0:T(8,128)(2,1)} %copy.24.right_w), custom_call_target="tpu_custom_call" | custom-call | bytes 524288 | tf_op jit(solution)/shard_map/project/pallas_call | solution.py:545
  6.1 3.0 %collective-permute-start.9 = (bf16[32,1024]{1,0:T(8,128)(2,1)}, bf16[32,1024]{1,0:T(8,128)(2,1)S(1)}, u32[]{:S(2)}, u32[]{:S(2)}) collective-permute-start(bf16[32,1024]{1,0:T(8,128)(2,1)} %get-tuple-element.32), channel_id=1, source_target_pairs={{1,0},{5,1},{3,2},{7,3},{0,4},{4,5},{2,6},{6,7},{9,8},{13,9},{11,1... | collective-permute-start | bytes 196616 | tf_op jit(solution)/shard_map/ppermute | solution.py:515
  9.1 1.5 %collective-permute-start.8 = (bf16[32,1024]{1,0:T(8,128)(2,1)}, bf16[32,1024]{1,0:T(8,128)(2,1)S(1)}, u32[]{:S(2)}, u32[]{:S(2)}) collective-permute-start(bf16[32,1024]{1,0:T(8,128)(2,1)} %get-tuple-element.32), channel_id=1, source_target_pairs={{0,0},{4,1},{2,2},{6,3},{1,4},{5,5},{3,6},{7,7},{8,8},{12,9},{10,1... | collective-permute-start | bytes 196616 | tf_op jit(solution)/shard_map/ppermute | solution.py:515
  10.6 3.4 %collective-permute-start.7 = (bf16[32,1024]{1,0:T(8,128)(2,1)}, bf16[32,1024]{1,0:T(8,128)(2,1)S(1)}, u32[]{:S(2)}, u32[]{:S(2)}) collective-permute-start(bf16[32,1024]{1,0:T(8,128)(2,1)} %get-tuple-element.31.left_own), channel_id=1, source_target_pairs={{1,0},{0,1},{3,2},{2,3},{5,4},{4,5},{7,6},{6,7},{9,8},{8,9},{11,10... | collective-permute-start | bytes 196616 | tf_op jit(solution)/shard_map/ppermute | solution.py:515
  14.1 0.0 collective-permute-done.9.p_two
  14.1 0.0 collective-permute-done.8.p_one
  14.1 0.5 collective-permute-start.10
  14.6 0.0 copy-start.29
  14.6 2.7 %collective-permute-start.12 = (bf16[4,32,128]{2,1,0:T(8,128)(2,1)S(1)}, bf16[4,32,128]{2,1,0:T(8,128)(2,1)S(1)}, u32[]{:S(2)}, u32[]{:S(2)}) collective-permute-start(bf16[4,32,128]{2,1,0:T(8,128)(2,1)S(1)} %maximum_bitcast_fusion.w_own), channel_id=1, source_target_pairs={{16,0},{17,1},{18,2},{19,3},{20,4},{21,5},{22,6},{23,7},{24,8},{25... | collective-permute-start | bytes 98312 | tf_op jit(solution)/shard_map/ppermute | solution.py:515
  17.3 0.6 pad.6.offset_t
  17.9 2.6 %pair.1 = (bf16[16,128,128]{2,1,0:T(8,128)(2,1)}, bf16[32,128]{1,0:T(8,128)(2,1)}, bf16[128,1024]{1,0:T(8,128)(2,1)}) custom-call(bf16[2048,128]{1,0:T(8,128)(2,1)} %bitcast.12, bf16[8,128]{1,0:T(8,128)(2,1)} %pad.6.offset_t, bf16[1024,128]{1,0:T(8,128)(2,1)} %outer_w.1), custom_call_target="tpu_custom_call" | custom-call | bytes 524288 | tf_op jit(solution)/shard_map/pair/pallas_call | solution.py:556
  20.5 0.0 collective-permute-done.7.left_far
  20.5 0.0 collective-permute-done.11.s_two
  20.6 0.5 copy-done.13
  21.1 0.0 copy-done.16
  21.1 0.0 copy-done.17
  21.2 0.0 copy-done.18
  21.2 7.8 %outer.1 = (bf16[16,128,128]{2,1,0:T(8,128)(2,1)}, bf16[16,128,128]{2,1,0:T(8,128)(2,1)}, bf16[1024,128]{1,0:T(8,128)(2,1)}) custom-call(bf16[16,128,128]{2,1,0:T(8,128)(2,1)} %get-tuple-element.29.couple_t, bf16[128,1024]{1,0:T(8,128)(2,1)} %get-tuple-element.30.outer_wt, bf16[32,1024]{1,0:T(8,128)(2,1)} %get-tuple-element.31.left_own, ...), custom_call_target="tpu_custom_call" | custom-call | bytes 524288 | tf_op jit(solution)/shard_map/outer/pallas_call | solution.py:578
  29.0 3.3 %collective-permute-start.14 = (bf16[1024,128]{1,0:T(8,128)(2,1)}, bf16[1024,128]{1,0:T(8,128)(2,1)S(1)}, u32[]{:S(2)}, u32[]{:S(2)}) collective-permute-start(bf16[1024,128]{1,0:T(8,128)(2,1)} %get-tuple-element.35.own), channel_id=1, source_target_pairs={{4,0},{5,1},{6,2},{7,3},{0,4},{1,5},{2,6},{3,7},{12,8},{13,9},{14,... | collective-permute-start | bytes 786440 | tf_op jit(solution)/shard_map/ppermute | solution.py:515
  32.3 6.9 %collective-permute-done.14.across = bf16[1024,128]{1,0:T(8,128)(2,1)S(1)} collective-permute-done((bf16[1024,128]{1,0:T(8,128)(2,1)}, bf16[1024,128]{1,0:T(8,128)(2,1)S(1)}, u32[]{:S(2)}, u32[]{:S(2)}) %collective-permute-start.14) | collective-permute-done | bytes 262176 | tf_op jit(solution)/shard_map/ppermute | solution.py:515
  39.2 0.0 collective-permute-start.15
  39.2 0.1 copy.27
  39.3 0.0 copy-start.21
  39.3 0.1 copy.25
  39.5 0.6 copy-done.21
  40.1 0.1 copy.26
  40.2 0.6 copy-done.22
  40.9 0.1 copy.28
  41.0 0.8 pad_maximum_fusion.weights
  41.8 2.2 %heads.1 = (bf16[1024,128]{1,0:T(8,128)(2,1)}, f32[1024,128]{1,0:T(8,128)}) custom-call(bf16[1024,256]{1,0:T(8,128)(2,1)} %get-tuple-element.21.normed, bf16[256,256]{1,0:T(8,128)(2,1)} %pad_maximum_fusion.weights), custom_call_target="tpu_custom_call" | custom-call | bytes 524288 | tf_op jit(solution)/shard_map/heads/pallas_call | solution.py:569
  44.0 1.7 %collective-permute-start.1 = (bf16[1024,128]{1,0:T(8,128)(2,1)}, bf16[1024,128]{1,0:T(8,128)(2,1)S(1)}, u32[]{:S(2)}, u32[]{:S(2)}) collective-permute-start(bf16[1024,128]{1,0:T(8,128)(2,1)} %get-tuple-element.23.own), channel_id=1, source_target_pairs={{4,0},{5,1},{6,2},{7,3},{0,4},{1,5},{2,6},{3,7},{12,8},{13,9},{14,... | collective-permute-start | bytes 786440 | tf_op jit(solution)/shard_map/ppermute | solution.py:515
  45.7 3.1 %left.1 = (bf16[1024,128]{1,0:T(8,128)(2,1)}, f32[16,128,128]{2,1,0:T(8,128)}) custom-call(bf16[16,128,128]{2,1,0:T(8,128)(2,1)} %get-tuple-element.33.norm_t, bf16[4,32,128]{2,1,0:T(8,128)(2,1)} %copy-done.1, bf16[4,32,128]{2,1,0:T(8,128)(2,1)} %copy-done.13, bf16[128,128]{1,0:T(8,128)(2,1)} %close_w.1), custom_call_target="tpu_custom_call" | custom-call | bytes 524288 | tf_op jit(solution)/shard_map/left/pallas_call | solution.py:595
  48.8 0.0 collective-permute-done.13.sib
  48.8 0.7 copy-done.3
  49.5 0.1 copy-done.4
  49.6 3.1 %triangle.1 = (f32[1024,128]{1,0:T(8,128)}, bf16[1024,128]{1,0:T(8,128)(2,1)}) custom-call(bf16[1024,128]{1,0:T(8,128)(2,1)} %get-tuple-element.34.left_pk, bf16[1024,128]{1,0:T(8,128)(2,1)} %get-tuple-element.35.own, bf16[1024,128]{1,0:T(8,128)(2,1)} %copy-done.3, bf16[1024,128]{1,0:T(8,128)(2,1)} %copy-done.2, bf16[1024,128]{1,0:T(8,128)(2,1)} %copy-done.4), custom_call_target="tpu_custom_call" | custom-call | bytes 524288 | tf_op jit(solution)/shard_map/triangle/pallas_call | solution.py:608
  52.7 0.0 collective-permute-start.16
  52.7 0.3 collective-permute-start
  53.0 0.0 collective-permute-done.1.across
  53.0 0.3 collective-permute-start.2
  53.3 8.1 %collective-permute-done.16 = bf16[1024,128]{1,0:T(8,128)(2,1)S(1)} collective-permute-done((bf16[1024,128]{1,0:T(8,128)(2,1)}, bf16[1024,128]{1,0:T(8,128)(2,1)S(1)}, u32[]{:S(2)}, u32[]{:S(2)}) %collective-permute-start.16) | collective-permute-done | bytes 262176 | tf_op jit(solution)/shard_map/ppermute | solution.py:515
  61.4 1.1 %add_convert_fusion.half_own = bf16[1024,128]{1,0:T(8,128)(2,1)S(1)} fusion(f32[1024,128]{1,0:T(8,128)} %get-tuple-element.36, bf16[1024,128]{1,0:T(8,128)(2,1)S(1)} %collective-permute-done.16), kind=kLoop, calls=%fused_computation | loop fusion | flops 393216 | bytes 1048576 | tf_op jit(solution)/shard_map/convert_element_type | solution.py:614
  62.5 1.6 %collective-permute-start.17 = (bf16[1024,128]{1,0:T(8,128)(2,1)S(1)}, bf16[1024,128]{1,0:T(8,128)(2,1)S(1)}, u32[]{:S(2)}, u32[]{:S(2)}) collective-permute-start(bf16[1024,128]{1,0:T(8,128)(2,1)S(1)} %add_convert_fusion.half_own), channel_id=1, source_target_pairs={{8,0},{9,1},{10,2},{11,3},{12,4},{13,5},{14,6},{15,7},{0,8},{1,9},... | collective-permute-start | bytes 786440 | tf_op jit(solution)/shard_map/ppermute | solution.py:515
  64.2 0.3 collective-permute-start.3
  64.4 0.1 reshape.21
  64.6 0.8 fusion.2.w_out
  65.3 2.5 %collective-permute-done.3.bias_far = bf16[32,128]{1,0:T(8,128)(2,1)S(1)} collective-permute-done((bf16[32,128]{1,0:T(8,128)(2,1)S(1)}, bf16[32,128]{1,0:T(8,128)(2,1)S(1)}, u32[]{:S(2)}, u32[]{:S(2)}) %collective-permute-start.3) | collective-permute-done | bytes 8224 | tf_op jit(solution)/shard_map/ppermute | solution.py:515
  67.8 0.6 copy-done.28
  68.4 0.1 copy-done.7
  68.5 0.1 copy-done.8
  68.6 11.1 %attend.1 = (bf16[512,128]{1,0:T(8,128)(2,1)}, bf16[512,128]{1,0:T(8,128)(2,1)}, bf16[512,128]{1,0:T(8,128)(2,1)}, bf16[512,128]{1,0:T(8,128)(2,1)}) custom-call(f32[1024,128]{1,0:T(8,128)} %get-tuple-element.22.qg, bf16[1024,128]{1,0:T(8,128)(2,1)} %get-tuple-element.23.own, bf16[1024,128]{1,0:T(8,128)(2,1)} %copy-done.7, bf16[1024,128]{1,0:T(8,128)(2,1)} %copy-done.6, ...), custom_call_target="tpu_custom_call" | custom-call | bytes 524288 | tf_op jit(solution)/shard_map/attend/pallas_call | solution.py:622
  79.7 0.5 collective-permute-start.4
  80.2 1.5 %collective-permute-start.5 = (bf16[512,128]{1,0:T(8,128)(2,1)}, bf16[512,128]{1,0:T(8,128)(2,1)S(1)}, u32[]{:S(2)}, u32[]{:S(2)}) collective-permute-start(bf16[512,128]{1,0:T(8,128)(2,1)} %get-tuple-element.27), channel_id=1, source_target_pairs={{16,0},{17,1},{18,2},{19,3},{20,4},{21,5},{22,6},{23,7},{24,8},{25... | collective-permute-start | bytes 393224 | tf_op jit(solution)/shard_map/ppermute | solution.py:515
  81.6 2.5 %collective-permute-start.6 = (bf16[512,128]{1,0:T(8,128)(2,1)}, bf16[512,128]{1,0:T(8,128)(2,1)S(1)}, u32[]{:S(2)}, u32[]{:S(2)}) collective-permute-start(bf16[512,128]{1,0:T(8,128)(2,1)} %get-tuple-element.28), channel_id=1, source_target_pairs={{24,0},{25,1},{26,2},{27,3},{28,4},{29,5},{30,6},{31,7},{16,8},{17... | collective-permute-start | bytes 393224 | tf_op jit(solution)/shard_map/ppermute | solution.py:515
  84.1 0.8 collective-permute-done.4.p1
  84.9 6.9 %collective-permute-done.5.p2 = bf16[512,128]{1,0:T(8,128)(2,1)S(1)} collective-permute-done((bf16[512,128]{1,0:T(8,128)(2,1)}, bf16[512,128]{1,0:T(8,128)(2,1)S(1)}, u32[]{:S(2)}, u32[]{:S(2)}) %collective-permute-start.5) | collective-permute-done | bytes 131104 | tf_op jit(solution)/shard_map/ppermute | solution.py:515
  91.9 0.6 copy-done.11
  92.5 0.1 copy-done.12
  92.6 2.2 %revise.1 = bf16[1024,64]{1,0:T(8,128)(2,1)} custom-call(bf16[1024,256]{1,0:T(8,128)(2,1)} %bitcast.11, bf16[512,128]{1,0:T(8,128)(2,1)} %get-tuple-element.25.p0, bf16[512,128]{1,0:T(8,128)(2,1)} %copy-done.10, bf16[512,128]{1,0:T(8,128)(2,1)} %copy-done.11, bf16[512,128]{1,0:T(8,128)(2,1)} %copy-done.12), custom_call_target="tpu_custom_call" | custom-call | bytes 524288 | tf_op jit(solution)/shard_map/revise/pallas_call | solution.py:631
  94.7 0.0 collective-permute-done.17.half_far
  94.7 0.7 copy-done.9
  95.4 3.8 %final.1 = bf16[2048,128]{1,0:T(8,128)(2,1)} custom-call(bf16[1024,128]{1,0:T(8,128)(2,1)} %copy-done, bf16[1024,128]{1,0:T(8,128)(2,1)} %copy-done.9, bf16[16,128,128]{2,1,0:T(8,128)(2,1)} %get-tuple-element.38.mid_t, f32[16,128,128]{2,1,0:T(8,128)} %get-tuple-element.39.close_t, bf16[128,128]{1,0:T(8,128)(2,1)} %final_w.1), custom_call_target="tpu_custom_call" | custom-call | bytes 524288 | tf_op jit(solution)/shard_map/final/pallas_call | solution.py:633
  (54 shorter events, 0.1 us)
Async XLA Ops:
  0.6 1.5 %copy-start.24 = (bf16[256,32]{0,1:T(8,128)(2,1)S(1)}, bf16[256,32]{0,1:T(8,128)(2,1)}, u32[]{:S(2)}) copy-start(bf16[256,32]{0,1:T(8,128)(2,1)} %param.24) | copy-start | bytes 49156
  2.8 11.8 %copy-start.25 = (bf16[2,128,32]{1,2,0:T(8,128)(2,1)S(1)}, bf16[2,128,32]{1,2,0:T(8,128)(2,1)}, u32[]{:S(2)}) copy-start(bf16[2,128,32]{1,2,0:T(8,128)(2,1)} %param.27) | copy-start | bytes 49156
  2.8 11.8 %copy-start.26 = (bf16[2,128,32]{1,2,0:T(8,128)(2,1)S(1)}, bf16[2,128,32]{1,2,0:T(8,128)(2,1)}, u32[]{:S(2)}) copy-start(bf16[2,128,32]{1,2,0:T(8,128)(2,1)} %param.26) | copy-start | bytes 49156
  6.1 7.9 %collective-permute-start.9 = (bf16[32,1024]{1,0:T(8,128)(2,1)}, bf16[32,1024]{1,0:T(8,128)(2,1)S(1)}, u32[]{:S(2)}, u32[]{:S(2)}) collective-permute-start(bf16[32,1024]{1,0:T(8,128)(2,1)} %get-tuple-element.32), channel_id=1, source_target_pairs={{1,0},{5,1},{3,2},{7,3},{0,4},{4,5},{2,6},{6,7},{9,8},{13,9},{11,1... | collective-permute-start | bytes 196616 | tf_op jit(solution)/shard_map/ppermute | solution.py:515
  9.1 4.9 %collective-permute-start.8 = (bf16[32,1024]{1,0:T(8,128)(2,1)}, bf16[32,1024]{1,0:T(8,128)(2,1)S(1)}, u32[]{:S(2)}, u32[]{:S(2)}) collective-permute-start(bf16[32,1024]{1,0:T(8,128)(2,1)} %get-tuple-element.32), channel_id=1, source_target_pairs={{0,0},{4,1},{2,2},{6,3},{1,4},{5,5},{3,6},{7,7},{8,8},{12,9},{10,1... | collective-permute-start | bytes 196616 | tf_op jit(solution)/shard_map/ppermute | solution.py:515
  10.6 9.9 %collective-permute-start.7 = (bf16[32,1024]{1,0:T(8,128)(2,1)}, bf16[32,1024]{1,0:T(8,128)(2,1)S(1)}, u32[]{:S(2)}, u32[]{:S(2)}) collective-permute-start(bf16[32,1024]{1,0:T(8,128)(2,1)} %get-tuple-element.31.left_own), channel_id=1, source_target_pairs={{1,0},{0,1},{3,2},{2,3},{5,4},{4,5},{7,6},{6,7},{9,8},{8,9},{11,10... | collective-permute-start | bytes 196616 | tf_op jit(solution)/shard_map/ppermute | solution.py:515
  14.1 6.4 %copy-start.14 = (bf16[32,1024]{1,0:T(8,128)(2,1)}, bf16[32,1024]{1,0:T(8,128)(2,1)S(1)}, u32[]{:S(2)}) copy-start(bf16[32,1024]{1,0:T(8,128)(2,1)S(1)} %collective-permute-done.9.p_two) | copy-start | bytes 196612
  14.1 6.4 %collective-permute-start.11 = (bf16[32,1024]{1,0:T(8,128)(2,1)S(1)}, bf16[32,1024]{1,0:T(8,128)(2,1)S(1)}, u32[]{:S(2)}, u32[]{:S(2)}) collective-permute-start(bf16[32,1024]{1,0:T(8,128)(2,1)S(1)} %collective-permute-done.9.p_two), channel_id=1, source_target_pairs={{2,0},{3,1},{0,2},{1,3},{6,4},{7,5},{4,6},{5,7},{10,8},{11,9},{8,1... | collective-permute-start | bytes 196616 | tf_op jit(solution)/shard_map/ppermute | solution.py:515
  14.1 6.4 %copy-start.15 = (bf16[32,1024]{1,0:T(8,128)(2,1)}, bf16[32,1024]{1,0:T(8,128)(2,1)S(1)}, u32[]{:S(2)}) copy-start(bf16[32,1024]{1,0:T(8,128)(2,1)S(1)} %collective-permute-done.8.p_one) | copy-start | bytes 196612
  14.1 6.4 %collective-permute-start.10 = (bf16[32,1024]{1,0:T(8,128)(2,1)S(1)}, bf16[32,1024]{1,0:T(8,128)(2,1)S(1)}, u32[]{:S(2)}, u32[]{:S(2)}) collective-permute-start(bf16[32,1024]{1,0:T(8,128)(2,1)S(1)} %collective-permute-done.8.p_one), channel_id=1, source_target_pairs={{2,0},{3,1},{0,2},{1,3},{6,4},{7,5},{4,6},{5,7},{10,8},{11,9},{8,1... | collective-permute-start | bytes 196616 | tf_op jit(solution)/shard_map/ppermute | solution.py:515
  14.6 5.9 %copy-start.1 = (bf16[4,32,128]{2,1,0:T(8,128)(2,1)}, bf16[4,32,128]{2,1,0:T(8,128)(2,1)S(1)}, u32[]{:S(2)}) copy-start(bf16[4,32,128]{2,1,0:T(8,128)(2,1)S(1)} %maximum_bitcast_fusion.w_own) | copy-start | bytes 98308
  14.6 2.7 %copy-start.29 = (bf16[128,2]{0,1:T(2,128)(2,1)S(1)}, bf16[128,2]{0,1:T(2,128)(2,1)}, u32[]{:S(2)}) copy-start(bf16[128,2]{0,1:T(2,128)(2,1)} %param.22) | copy-start | bytes 1540
  14.6 5.9 %collective-permute-start.12 = (bf16[4,32,128]{2,1,0:T(8,128)(2,1)S(1)}, bf16[4,32,128]{2,1,0:T(8,128)(2,1)S(1)}, u32[]{:S(2)}, u32[]{:S(2)}) collective-permute-start(bf16[4,32,128]{2,1,0:T(8,128)(2,1)S(1)} %maximum_bitcast_fusion.w_own), channel_id=1, source_target_pairs={{16,0},{17,1},{18,2},{19,3},{20,4},{21,5},{22,6},{23,7},{24,8},{25... | collective-permute-start | bytes 98312 | tf_op jit(solution)/shard_map/ppermute | solution.py:515
  20.5 0.6 copy-start.13
  20.5 0.6 copy-start.16
  20.5 0.6 copy-start.17
  20.5 0.7 copy-start.18
  21.2 18.0 %copy-start.19 = (bf16[256,64]{0,1:T(8,128)(2,1)S(1)}, bf16[256,64]{0,1:T(8,128)(2,1)}, u32[]{:S(2)}) copy-start(bf16[256,64]{0,1:T(8,128)(2,1)} %param.17) | copy-start | bytes 98308
  29.0 10.3 %copy-start.20 = (bf16[256,64]{0,1:T(8,128)(2,1)S(1)}, bf16[256,64]{0,1:T(8,128)(2,1)}, u32[]{:S(2)}) copy-start(bf16[256,64]{0,1:T(8,128)(2,1)} %param.18) | copy-start | bytes 98308
  29.0 10.2 %collective-permute-start.14 = (bf16[1024,128]{1,0:T(8,128)(2,1)}, bf16[1024,128]{1,0:T(8,128)(2,1)S(1)}, u32[]{:S(2)}, u32[]{:S(2)}) collective-permute-start(bf16[1024,128]{1,0:T(8,128)(2,1)} %get-tuple-element.35.own), channel_id=1, source_target_pairs={{4,0},{5,1},{6,2},{7,3},{0,4},{1,5},{2,6},{3,7},{12,8},{13,9},{14,... | collective-permute-start | bytes 786440 | tf_op jit(solution)/shard_map/ppermute | solution.py:515
  32.3 16.5 %collective-permute-start.13 = (bf16[1024,128]{1,0:T(8,128)(2,1)}, bf16[1024,128]{1,0:T(8,128)(2,1)S(1)}, u32[]{:S(2)}, u32[]{:S(2)}) collective-permute-start(bf16[1024,128]{1,0:T(8,128)(2,1)} %get-tuple-element.35.own), channel_id=1, source_target_pairs={{2,0},{3,1},{0,2},{1,3},{6,4},{7,5},{4,6},{5,7},{10,8},{11,9},{8,1... | collective-permute-start | bytes 786440 | tf_op jit(solution)/shard_map/ppermute | solution.py:515
  39.2 2.6 %copy-start.2 = (bf16[1024,128]{1,0:T(8,128)(2,1)}, bf16[1024,128]{1,0:T(8,128)(2,1)S(1)}, u32[]{:S(2)}) copy-start(bf16[1024,128]{1,0:T(8,128)(2,1)S(1)} %collective-permute-done.14.across) | copy-start | bytes 786436
  39.2 9.6 %collective-permute-start.15 = (bf16[1024,128]{1,0:T(8,128)(2,1)S(1)}, bf16[1024,128]{1,0:T(8,128)(2,1)S(1)}, u32[]{:S(2)}, u32[]{:S(2)}) collective-permute-start(bf16[1024,128]{1,0:T(8,128)(2,1)S(1)} %collective-permute-done.14.across), channel_id=1, source_target_pairs={{2,0},{3,1},{0,2},{1,3},{6,4},{7,5},{4,6},{5,7},{10,8},{11,9},{8,1... | collective-permute-start | bytes 786440 | tf_op jit(solution)/shard_map/ppermute | solution.py:515
  39.3 0.8 copy-start.21
  40.1 0.8 copy-start.22
  44.0 9.0 %collective-permute-start.1 = (bf16[1024,128]{1,0:T(8,128)(2,1)}, bf16[1024,128]{1,0:T(8,128)(2,1)S(1)}, u32[]{:S(2)}, u32[]{:S(2)}) collective-permute-start(bf16[1024,128]{1,0:T(8,128)(2,1)} %get-tuple-element.23.own), channel_id=1, source_target_pairs={{4,0},{5,1},{6,2},{7,3},{0,4},{1,5},{2,6},{3,7},{12,8},{13,9},{14,... | collective-permute-start | bytes 786440 | tf_op jit(solution)/shard_map/ppermute | solution.py:515
  48.8 0.7 copy-start.3
  48.8 0.8 copy-start.4
  49.6 3.1 %copy-start.5 = (bf16[1024,128]{1,0:T(8,128)(2,1)S(1)}, bf16[1024,128]{1,0:T(8,128)(2,1)}, u32[]{:S(2)}) copy-start(bf16[1024,128]{1,0:T(8,128)(2,1)} %get-tuple-element.23.own) | copy-start | bytes 786436
  52.7 8.7 %collective-permute-start.16 = (bf16[1024,128]{1,0:T(8,128)(2,1)}, bf16[1024,128]{1,0:T(8,128)(2,1)S(1)}, u32[]{:S(2)}, u32[]{:S(2)}) collective-permute-start(bf16[1024,128]{1,0:T(8,128)(2,1)} %get-tuple-element.37), channel_id=1, source_target_pairs={{1,0},{0,1},{3,2},{2,3},{5,4},{4,5},{7,6},{6,7},{9,8},{8,9},{11,10... | collective-permute-start | bytes 786440 | tf_op jit(solution)/shard_map/ppermute | solution.py:515
  52.7 15.1 %collective-permute-start = (bf16[1024,128]{1,0:T(8,128)(2,1)S(1)}, bf16[1024,128]{1,0:T(8,128)(2,1)S(1)}, u32[]{:S(2)}, u32[]{:S(2)}) collective-permute-start(bf16[1024,128]{1,0:T(8,128)(2,1)S(1)} %copy-done.5), channel_id=1, source_target_pairs={{2,0},{3,1},{0,2},{1,3},{6,4},{7,5},{4,6},{5,7},{10,8},{11,9},{8,1... | collective-permute-start | bytes 786440 | tf_op jit(solution)/shard_map/ppermute | solution.py:515
  53.0 9.5 %copy-start.6 = (bf16[1024,128]{1,0:T(8,128)(2,1)}, bf16[1024,128]{1,0:T(8,128)(2,1)S(1)}, u32[]{:S(2)}) copy-start(bf16[1024,128]{1,0:T(8,128)(2,1)S(1)} %collective-permute-done.1.across) | copy-start | bytes 786436
  53.0 14.8 %collective-permute-start.2 = (bf16[1024,128]{1,0:T(8,128)(2,1)S(1)}, bf16[1024,128]{1,0:T(8,128)(2,1)S(1)}, u32[]{:S(2)}, u32[]{:S(2)}) collective-permute-start(bf16[1024,128]{1,0:T(8,128)(2,1)S(1)} %collective-permute-done.1.across), channel_id=1, source_target_pairs={{2,0},{3,1},{0,2},{1,3},{6,4},{7,5},{4,6},{5,7},{10,8},{11,9},{8,1... | collective-permute-start | bytes 786440 | tf_op jit(solution)/shard_map/ppermute | solution.py:515
  61.4 2.8 %copy-start.27 = (bf16[32,128]{1,0:T(8,128)(2,1)S(1)}, bf16[32,128]{1,0:T(8,128)(2,1)}, u32[]{:S(2)}) copy-start(bf16[32,128]{1,0:T(8,128)(2,1)} %get-tuple-element.24.bias_own) | copy-start | bytes 24580
  61.4 3.1 %copy-start.23 = (bf16[64,256]{1,0:T(8,128)(2,1)S(1)}, bf16[64,256]{1,0:T(8,128)(2,1)}, u32[]{:S(2)}) copy-start(bf16[64,256]{1,0:T(8,128)(2,1)} %param.21) | copy-start | bytes 98308
  62.5 17.2 %copy-start = (bf16[1024,128]{1,0:T(8,128)(2,1)}, bf16[1024,128]{1,0:T(8,128)(2,1)S(1)}, u32[]{:S(2)}) copy-start(bf16[1024,128]{1,0:T(8,128)(2,1)S(1)} %add_convert_fusion.half_own) | copy-start | bytes 786436
  62.5 32.2 %collective-permute-start.17 = (bf16[1024,128]{1,0:T(8,128)(2,1)S(1)}, bf16[1024,128]{1,0:T(8,128)(2,1)S(1)}, u32[]{:S(2)}, u32[]{:S(2)}) collective-permute-start(bf16[1024,128]{1,0:T(8,128)(2,1)S(1)} %add_convert_fusion.half_own), channel_id=1, source_target_pairs={{8,0},{9,1},{10,2},{11,3},{12,4},{13,5},{14,6},{15,7},{0,8},{1,9},... | collective-permute-start | bytes 786440 | tf_op jit(solution)/shard_map/ppermute | solution.py:515
  64.2 3.7 %collective-permute-start.3 = (bf16[32,128]{1,0:T(8,128)(2,1)S(1)}, bf16[32,128]{1,0:T(8,128)(2,1)S(1)}, u32[]{:S(2)}, u32[]{:S(2)}) collective-permute-start(bf16[32,128]{1,0:T(8,128)(2,1)S(1)} %copy-done.27), channel_id=1, source_target_pairs={{1,0},{0,1},{3,2},{2,3},{5,4},{4,5},{7,6},{6,7},{9,8},{8,9},{11,10... | collective-permute-start | bytes 24584 | tf_op jit(solution)/shard_map/ppermute | solution.py:515
  67.8 0.6 copy-start.28
  67.8 0.7 copy-start.7
  67.8 0.8 copy-start.8
  79.7 5.2 %collective-permute-start.4 = (bf16[512,128]{1,0:T(8,128)(2,1)}, bf16[512,128]{1,0:T(8,128)(2,1)S(1)}, u32[]{:S(2)}, u32[]{:S(2)}) collective-permute-start(bf16[512,128]{1,0:T(8,128)(2,1)} %get-tuple-element.26), channel_id=1, source_target_pairs={{8,0},{9,1},{10,2},{11,3},{12,4},{13,5},{14,6},{15,7},{0,8},{1,9},... | collective-permute-start | bytes 393224 | tf_op jit(solution)/shard_map/ppermute | solution.py:515
  80.2 11.7 %collective-permute-start.5 = (bf16[512,128]{1,0:T(8,128)(2,1)}, bf16[512,128]{1,0:T(8,128)(2,1)S(1)}, u32[]{:S(2)}, u32[]{:S(2)}) collective-permute-start(bf16[512,128]{1,0:T(8,128)(2,1)} %get-tuple-element.27), channel_id=1, source_target_pairs={{16,0},{17,1},{18,2},{19,3},{20,4},{21,5},{22,6},{23,7},{24,8},{25... | collective-permute-start | bytes 393224 | tf_op jit(solution)/shard_map/ppermute | solution.py:515
  81.6 10.2 %collective-permute-start.6 = (bf16[512,128]{1,0:T(8,128)(2,1)}, bf16[512,128]{1,0:T(8,128)(2,1)S(1)}, u32[]{:S(2)}, u32[]{:S(2)}) collective-permute-start(bf16[512,128]{1,0:T(8,128)(2,1)} %get-tuple-element.28), channel_id=1, source_target_pairs={{24,0},{25,1},{26,2},{27,3},{28,4},{29,5},{30,6},{31,7},{16,8},{17... | collective-permute-start | bytes 393224 | tf_op jit(solution)/shard_map/ppermute | solution.py:515
  84.9 7.0 %copy-start.10 = (bf16[512,128]{1,0:T(8,128)(2,1)}, bf16[512,128]{1,0:T(8,128)(2,1)S(1)}, u32[]{:S(2)}) copy-start(bf16[512,128]{1,0:T(8,128)(2,1)S(1)} %collective-permute-done.4.p1) | copy-start | bytes 393220
  91.9 0.7 copy-start.11
  91.9 0.7 copy-start.12
  94.7 0.7 copy-start.9
